TPU v7x, 256 devices: a whole 4x4x8 slice. The times are simulated.
256 devices in a mesh: section: 4 (over x_hi, core), dp: 64 (over y, x_lo, z).
Axes of the slice: x: 4 (x_hi: 2, x_lo: 2; x = x_hi * 2 + x_lo), y: 4, z: 8, core: 2. Of those that a mesh axis runs over, the one named last changes fastest.
Arguments:
- activations: bfloat16 [12288, 8, 4096], P('dp', 'section'), may hold values from -8 to 8
- damping: float32 [8], P('section'), may hold values from 0.1 to 1
Outputs:
- schur_inverse: float32 [256, 128, 128], P(('section', 'dp'))
- coupling: float32 [256, 128, 128], P(('section', 'dp'))
All inputs are finite; a program needn't handle non-finite values.
Results may differ from a plain program's by a relative error of at most 0.0003.
Values may be sent and summed in bfloat16 or wider, within the bound.
A program may use at most 64 MiB of HBM per device.

v0:
```python
import jax
import jax.numpy as jnp
from jax import lax
from jax.sharding import PartitionSpec as P

B = 128


def passed_along(block, axis, distance):
    devices = range(lax.axis_size(axis))
    route = [(i - distance, i) for i in devices if i - distance in devices]
    return lax.ppermute(block, axis, route)


def sent_to_all(array, axis):
    copies = jnp.broadcast_to(array, (lax.axis_size(axis), *array.shape))
    return lax.all_to_all(copies, axis, split_axis=0, concat_axis=0, tiled=True)


def over_copies(array, axis):
    everything = sent_to_all(array, axis)
    return jnp.sum(everything, axis=0)


def solve_block(system, right_side):
    factor = jnp.linalg.cholesky(system)
    return jax.scipy.linalg.cho_solve((factor, True), right_side)


def local(activations, damping):
    token_rows, local_layers, model_width = activations.shape
    block_size = B
    blocks_layer = model_width // block_size
    group_size = lax.axis_size("dp")
    section_count = lax.axis_size("section")
    per_device = local_layers * blocks_layer // group_size
    tokens_all = token_rows * group_size
    flattened = activations.reshape(token_rows, local_layers * model_width)
    following_rows = passed_along(flattened[:, :model_width], "section", -1)
    next_layers = jnp.concatenate([flattened[:, model_width:], following_rows], axis=1)
    owner_layer = lax.axis_index("dp") * per_device // blocks_layer
    layer_index = jnp.arange(local_layers)
    sent_pairs = (
        flattened.reshape(token_rows, group_size, per_device * block_size),
        next_layers.reshape(token_rows, group_size, per_device * block_size),
    )
    left_cols, right_cols = (
        lax.all_to_all(sent_pairs[0], "dp", split_axis=1, concat_axis=0, tiled=True),
        lax.all_to_all(sent_pairs[1], "dp", split_axis=1, concat_axis=0, tiled=True),
    )
    diagonal_gram = (
        jnp.einsum("tgb,tgc->gbc", left_cols, left_cols, preferred_element_type=jnp.float32)
        / tokens_all
    )
    cross_gram = (
        jnp.einsum("tgb,tgc->gbc", left_cols, right_cols, preferred_element_type=jnp.float32)
        / tokens_all
    )
    owned_trace = jnp.sum(jnp.trace(diagonal_gram, axis1=1, axis2=2))
    traces = over_copies(jnp.where(layer_index == owner_layer, owned_trace, 0.0), "dp")
    identity = jnp.eye(block_size, dtype=jnp.float32)
    damp_level = jnp.sum(jnp.where(layer_index == owner_layer, traces * damping, 0.0)) / model_width
    damped = diagonal_gram + damp_level * identity
    following_damped = passed_along(damped, ("section", "dp"), -(group_size // local_layers))
    final_layer = jnp.logical_and(
        lax.axis_index("section") == section_count - 1, owner_layer == local_layers - 1
    )
    system = jnp.where(final_layer, identity, following_damped)
    cross_gram = jnp.where(final_layer, jnp.zeros_like(cross_gram), cross_gram)
    coupling_t = jax.vmap(solve_block)(system, jnp.swapaxes(cross_gram, 1, 2))
    schur = damped - jnp.matmul(cross_gram, coupling_t, precision=lax.Precision.HIGHEST)
    identities = jnp.broadcast_to(identity, schur.shape)
    schur_inverse = jax.vmap(solve_block)(schur, identities)
    return (schur_inverse, jnp.swapaxes(coupling_t, 1, 2))


def solution(mesh):
    placed = (P("dp", "section", None), P("section"))
    return jax.shard_map(
        local,
        mesh=mesh,
        in_specs=placed,
        out_specs=(P(("section", "dp"), None, None), P(("section", "dp"), None, None)),
        check_vma=False,
    )
```

profile of v0, /device:TPU:4, one launch (start us, length us, event | category | flops | bytes accessed | tf_op | source)
XLA Modules:
  0.0 224.7 jit_solution(8540265799306868774)
XLA Ops:
  0.6 4.8 %reshape_reshape.3 = bf16[192,64,128]{2,1,0:T(8,128)(2,1)S(1)} reshape(bf16[192,2,4096]{2,1,0:T(2,128)(2,1)} %param.5) | data formatting | bytes 6291456 | tf_op jit(solution)/shard_map/reshape;reshape | solution.py:44
  5.4 3.7 %copy.26 = bf16[192,64,128]{2,0,1:T(8,128)(2,1)} copy(bf16[192,64,128]{2,1,0:T(8,128)(2,1)S(1)} %reshape_reshape.3) | data formatting | bytes 6291456 | tf_op jit(solution)/shard_map/reshape;reshape | solution.py:44
  9.2 13.2 %all-to-all-start = ((bf16[192,64,128]{2,0,1:T(8,128)(2,1)}), bf16[192,64,128]{2,0,1:T(8,128)(2,1)}, u32[]{:S(2)}, u32[]{:S(2)}) async-start(bf16[192,64,128]{2,0,1:T(8,128)(2,1)} %copy.26), calls=%async_computation | async-start | bytes 6291456 | tf_op jit(solution)/shard_map/all_to_all | solution.py:48
  22.4 2.1 copy.42
  24.7 1.9 collective-permute-start
  26.7 70.0 %all-to-all-done = bf16[192,64,128]{2,0,1:T(8,128)(2,1)} async-done(((bf16[192,64,128]{2,0,1:T(8,128)(2,1)}), bf16[192,64,128]{2,0,1:T(8,128)(2,1)}, u32[]{:S(2)}, u32[]{:S(2)}) %all-to-all-start) | async-done | bytes 3145760 | tf_op jit(solution)/shard_map/all_to_all | solution.py:48
  96.7 4.5 %select_reduce_fusion.1 = (f32[]{:T(128)}, f32[128,128]{0,1:T(8,128)S(1)}) fusion(bf16[192,64,128]{2,0,1:T(8,128)(2,1)} %all-to-all-done), kind=kOutput, calls=%fused_computation.38 | convolution fusion | flops 402718720 | bytes 3211268 | tf_op jit(solution)/shard_map/tgb,tgc->gbc/dot_general | solution.py:52
  101.2 0.6 compare_select_fusion.1
  102.5 5.5 %all-to-all-start.1 = ((f32[64,1,2]{2,1,0:T(1,128)}), f32[64,1,2]{2,1,0:T(1,128)S(1)}, u32[]{:S(2)}, u32[]{:S(2)}) async-start(f32[64,1,2]{2,1,0:T(1,128)} %broadcast_in_dim.31), calls=%async_computation.1 | async-start | bytes 65536 | tf_op jit(solution)/shard_map/all_to_all | solution.py:17
  108.0 4.0 %copy_bitcast_fusion = bf16[192,64,128]{2,0,1:T(8,128)(2,1)} fusion(bf16[192,4096]{1,0:T(8,128)(2,1)} %collective-permute-done, bf16[192,4096]{1,0:T(8,128)(2,1)S(1)} %get-tuple-element.12), kind=kLoop, calls=%fused_computation | loop fusion | flops 6291456 | bytes 6291456 | tf_op jit(solution)/shard_map/reshape | solution.py:45
  112.0 6.3 %all-to-all-done.1 = f32[64,1,2]{2,1,0:T(1,128)S(1)} async-done(((f32[64,1,2]{2,1,0:T(1,128)}), f32[64,1,2]{2,1,0:T(1,128)S(1)}, u32[]{:S(2)}, u32[]{:S(2)}) %all-to-all-start.1) | async-done | bytes 544 | tf_op jit(solution)/shard_map/all_to_all | solution.py:17
  118.4 5.0 %all-to-all-start.2 = ((bf16[192,64,128]{2,0,1:T(8,128)(2,1)}), bf16[192,64,128]{2,0,1:T(8,128)(2,1)S(1)}, u32[]{:S(2)}, u32[]{:S(2)}) async-start(bf16[192,64,128]{2,0,1:T(8,128)(2,1)} %copy_bitcast_fusion), calls=%async_computation.2 | async-start | bytes 6291456 | tf_op jit(solution)/shard_map/all_to_all | solution.py:49
  124.8 3.6 %collective-permute-start.1 = (f32[1,128,128]{1,2,0:T(8,128)S(1)}, f32[1,128,128]{1,2,0:T(8,128)S(1)}, u32[]{:S(2)}, u32[]{:S(2)}) collective-permute-start(f32[1,128,128]{1,2,0:T(8,128)S(1)} %fusion.39), channel_id=1, source_target_pairs={{32,0},{33,1},{34,2},{35,3},{36,4},{37,5},{38,6},{39,7},{40,8},{41... | collective-permute-start | bytes 196616 | tf_op jit(solution)/shard_map/ppermute | solution.py:12
  128.4 5.2 %collective-permute-done.1 = f32[1,128,128]{1,2,0:T(8,128)S(1)} collective-permute-done((f32[1,128,128]{1,2,0:T(8,128)S(1)}, f32[1,128,128]{1,2,0:T(8,128)S(1)}, u32[]{:S(2)}, u32[]{:S(2)}) %collective-permute-start.1) | collective-permute-done | bytes 65568 | tf_op jit(solution)/shard_map/ppermute | solution.py:12
  133.8 11.7 %custom-call.10 = f32[1,128,128]{2,1,0:T(8,128)S(1)} custom-call(f32[1,128,128]{2,1,0:T(8,128)S(1)} %fusion.36), custom_call_target="Cholesky" | custom-call | tf_op jit(solution)/shard_map/vmap(jit(cholesky))/cholesky | solution.py:26
  146.2 0.7 fusion.26
  146.9 9.8 %custom-call.11 = f32[1,1,128,128]{2,3,1,0:T(8,128)S(1)} custom-call(f32[1,1,128,128]{3,2,1,0:T(8,128)S(1)} %fusion.26), custom_call_target="InvertDiagBlocksLowerTriangular" | custom-call | tf_op jit(solution)/shard_map/vmap(jit(_cho_solve))/triangular_solve | solution.py:27
  156.7 39.4 %all-to-all-done.2 = bf16[192,64,128]{2,0,1:T(8,128)(2,1)S(1)} async-done(((bf16[192,64,128]{2,0,1:T(8,128)(2,1)}), bf16[192,64,128]{2,0,1:T(8,128)(2,1)S(1)}, u32[]{:S(2)}, u32[]{:S(2)}) %all-to-all-start.2) | async-done | bytes 3145760 | tf_op jit(solution)/shard_map/all_to_all | solution.py:49
  196.1 3.0 %fusion.21 = f32[128,128]{0,1:T(8,128)S(1)} fusion(bf16[192,64,128]{2,0,1:T(8,128)(2,1)} %all-to-all-done, bf16[192,64,128]{2,0,1:T(8,128)(2,1)S(1)} %all-to-all-done.2, pred[]{:T(512)S(6)} %and.11), kind=kOutput, calls=%fused_computation.13 | convolution fusion | flops 402685952 | bytes 6356993 | tf_op jit(solution)/shard_map/tgb,tgc->gbc/dot_general | solution.py:56
  200.0 11.7 %custom-call.12 = f32[1,128,128]{2,1,0:T(8,128)S(1)} custom-call(f32[1,128,128]{2,1,0:T(8,128)S(1)} %fusion.29), custom_call_target="Cholesky" | custom-call | tf_op jit(solution)/shard_map/vmap(jit(cholesky))/cholesky | solution.py:26
  212.4 0.7 fusion.27
  213.1 9.8 %custom-call.13 = f32[1,1,128,128]{2,3,1,0:T(8,128)S(1)} custom-call(f32[1,1,128,128]{3,2,1,0:T(8,128)S(1)} %fusion.27), custom_call_target="InvertDiagBlocksLowerTriangular" | custom-call | tf_op jit(solution)/shard_map/vmap(jit(_cho_solve))/triangular_solve | solution.py:27
  223.2 0.8 convolution_bitcast_fusion
  224.0 0.7 copy.34
  (23 shorter events, 4.2 us)
Async XLA Ops:
  9.2 13.2 %copy-start = (bf16[192,2,4096]{2,1,0:T(2,128)(2,1)S(1)}, bf16[192,2,4096]{2,1,0:T(2,128)(2,1)}, u32[]{:S(2)}) copy-start(bf16[192,2,4096]{2,1,0:T(2,128)(2,1)} %param.5) | copy-start | bytes 9437188
  9.2 87.5 %all-to-all-start = ((bf16[192,64,128]{2,0,1:T(8,128)(2,1)}), bf16[192,64,128]{2,0,1:T(8,128)(2,1)}, u32[]{:S(2)}, u32[]{:S(2)}) async-start(bf16[192,64,128]{2,0,1:T(8,128)(2,1)} %copy.26), calls=%async_computation | async-start | bytes 6291456 | tf_op jit(solution)/shard_map/all_to_all | solution.py:48
  24.7 83.3 %collective-permute-start = (bf16[192,4096]{1,0:T(8,128)(2,1)S(1)}, bf16[192,4096]{1,0:T(8,128)(2,1)}, u32[]{:S(2)}, u32[]{:S(2)}) collective-permute-start(bf16[192,4096]{1,0:T(8,128)(2,1)S(1)} %get-tuple-element.13), channel_id=1, source_target_pairs={{64,0},{128,64},{192,128},{65,1},{129,65},{193,129},{66,2},{130,66... | collective-permute-start | bytes 4718600 | tf_op jit(solution)/shard_map/ppermute | solution.py:12
  102.5 15.9 %all-to-all-start.1 = ((f32[64,1,2]{2,1,0:T(1,128)}), f32[64,1,2]{2,1,0:T(1,128)S(1)}, u32[]{:S(2)}, u32[]{:S(2)}) async-start(f32[64,1,2]{2,1,0:T(1,128)} %broadcast_in_dim.31), calls=%async_computation.1 | async-start | bytes 65536 | tf_op jit(solution)/shard_map/all_to_all | solution.py:17
  112.0 11.5 %copy-start.1 = (f32[2]{0:T(128)S(1)}, f32[2]{0:T(128)}, u32[]{:S(2)}) copy-start(f32[2]{0:T(128)} %param.6) | copy-start | bytes 28
  118.4 77.8 %all-to-all-start.2 = ((bf16[192,64,128]{2,0,1:T(8,128)(2,1)}), bf16[192,64,128]{2,0,1:T(8,128)(2,1)S(1)}, u32[]{:S(2)}, u32[]{:S(2)}) async-start(bf16[192,64,128]{2,0,1:T(8,128)(2,1)} %copy_bitcast_fusion), calls=%async_computation.2 | async-start | bytes 6291456 | tf_op jit(solution)/shard_map/all_to_all | solution.py:49
  124.8 8.9 %collective-permute-start.1 = (f32[1,128,128]{1,2,0:T(8,128)S(1)}, f32[1,128,128]{1,2,0:T(8,128)S(1)}, u32[]{:S(2)}, u32[]{:S(2)}) collective-permute-start(f32[1,128,128]{1,2,0:T(8,128)S(1)} %fusion.39), channel_id=1, source_target_pairs={{32,0},{33,1},{34,2},{35,3},{36,4},{37,5},{38,6},{39,7},{40,8},{41... | collective-permute-start | bytes 196616 | tf_op jit(solution)/shard_map/ppermute | solution.py:12
where the time goes:
time: 225 us
  waiting for transfers between devices  121 us (54%)
  other arithmetic  51.1 us (23%)
  starting transfers between devices  29.4 us (13%)
  local copies, waits for them, and re-layouts  12.4 us (6%)
  matrix products  9.39 us (4%)
    all_to_all x1, waiting for transfers between devices, local(): lax.all_to_all(sent_pairs[0], 'dp', split_axis=1, concat_axis=0, tiled=True)  70 us
    all_to_all x1, waiting for transfers between devices, local(): lax.all_to_all(sent_pairs[1], 'dp', split_axis=1, concat_axis=0, tiled=True)  39.4 us
    another operation x6, other arithmetic, solve_block(): factor = jnp.linalg.cholesky(system)  24.8 us
    another operation x4, other arithmetic, solve_block(): return jax.scipy.linalg.cho_solve((factor, True), right_side)  20.9 us
    all_to_all x1, starting transfers between devices, local(): lax.all_to_all(sent_pairs[0], 'dp', split_axis=1, concat_axis=0, tiled=True)  13.2 us
    another operation x2, local copies, waits for them, and re-layouts, local(): flattened.reshape(token_rows, group_size, per_device * block_size)  8.53 us
    all_to_all x1, waiting for transfers between devices, sent_to_all(): return lax.all_to_all(copies, axis, split_axis=0, concat_axis=0, tiled=True)  6.34 us
    ppermute x2, starting transfers between devices, passed_along(): return lax.ppermute(block, axis, route)  5.55 us
  transfers between devices with their start and end apart: 5, of which 4 were waited for; matrix products, arithmetic and copies ran while one was open for 16% of the time, Pallas kernels for 0%

commit v1 on v0

--- a/solution.py
+++ b/solution.py
@@ -2,6 +2,7 @@
 import jax.numpy as jnp
 from jax import lax
 from jax.sharding import PartitionSpec as P
+from jax.lax import all_to_all, axis_size
 
 B = 128
 
@@ -46,7 +47,15 @@
     )
     left_cols, right_cols = (
         lax.all_to_all(sent_pairs[0], "dp", split_axis=1, concat_axis=0, tiled=True),
-        lax.all_to_all(sent_pairs[1], "dp", split_axis=1, concat_axis=0, tiled=True),
+        jnp.concatenate(
+            all_to_all(
+                jnp.stack(jnp.split(sent_pairs[1], axis_size("dp"), axis=1)),
+                split_axis=0,
+                concat_axis=0,
+                axis_name="dp",
+            ),
+            axis=0,
+        ),
     )
     diagonal_gram = (
         jnp.einsum("tgb,tgc->gbc", left_cols, left_cols, preferred_element_type=jnp.float32)

time: 225 us -> 234 us (1.040)
  local copies, waits for them, and re-layouts: 12.4 us -> 64.6 us
  waiting for transfers between devices: 121 us -> 80 us
  matrix products: 9.39 us -> 6.43 us
    all_to_all x1, waiting for transfers between devices: 70 us -> 26.7 us  [local(): lax.all_to_all(sent_pairs[0], 'dp', split_axis=1, concat_axis=0, tiled=True)]
    unnamed x6 -> x70, local copies, waits for them, and re-layouts: 2.82 us -> 44.8 us
    split x0 -> x4, local copies, waits for them, and re-layouts: none -> 6.49 us  [local(): jnp.split(sent_pairs[1], axis_size('dp'), axis=1)]
    reshape x1 -> x0, other arithmetic: 4 us -> none  [local(): next_layers.reshape(token_rows, group_size, per_device * block_size)]
    all_to_all x1, waiting for transfers between devices: 6.34 us -> 9.72 us  [sent_to_all(): return lax.all_to_all(copies, axis, split_axis=0, concat_axis=0, tiled=True)]
    dot_general x1, matrix products: 4.51 us -> 1.62 us  [local(): jnp.einsum('tgb,tgc->gbc', left_cols, left_cols, preferred_element_type=j...]
  transfers between devices with their start and end apart: 5 -> 5, of which waited for: 4 -> 4; matrix products, arithmetic and copies ran while one was open for 16% -> 36% of each run, Pallas kernels for 0% -> 0%
where the time goes in v1:
time: 234 us; the launch traced here: 233 us
  waiting for transfers between devices  80 us (34%)
  local copies, waits for them, and re-layouts  64.6 us (28%)
  other arithmetic  49.2 us (21%)
  starting transfers between devices  30.7 us (13%)
  matrix products  6.43 us (3%)
    unnamed x70, local copies, waits for them, and re-layouts  44.8 us
    all_to_all x1, waiting for transfers between devices, local(): all_to_all(jnp.stack(jnp.split(sent_pairs[1], axis_size('dp'), axis=1)),...  39.2 us
    all_to_all x1, waiting for transfers between devices, local(): lax.all_to_all(sent_pairs[0], 'dp', split_axis=1, concat_axis=0, tiled=True)  26.7 us
    another operation x6, other arithmetic, solve_block(): factor = jnp.linalg.cholesky(system)  24.8 us
    another operation x4, other arithmetic, solve_block(): return jax.scipy.linalg.cho_solve((factor, True), right_side)  20.9 us
    all_to_all x1, starting transfers between devices, local(): lax.all_to_all(sent_pairs[0], 'dp', split_axis=1, concat_axis=0, tiled=True)  13.8 us
    all_to_all x1, waiting for transfers between devices, sent_to_all(): return lax.all_to_all(copies, axis, split_axis=0, concat_axis=0, tiled=True)  9.72 us
    another operation x2, local copies, waits for them, and re-layouts, local(): flattened.reshape(token_rows, group_size, per_device * block_size)  9.62 us
  transfers between devices with their start and end apart: 5, of which 4 were waited for; matrix products, arithmetic and copies ran while one was open for 36% of the time, Pallas kernels for 0%

profile of v1, /device:TPU:4, one launch (start us, length us, event | category | flops | bytes accessed | tf_op | source)
XLA Modules:
  0.0 232.6 jit_solution(6855993180507538318)
XLA Ops:
  0.6 4.0 %copy.1862 = bf16[24,8,2,4096]{3,1,2,0:T(8,128)(2,1)S(1)} copy(bf16[24,8,2,4096]{3,2,1,0:T(2,128)(2,1)} %bitcast.222) | data formatting | bytes 6291456
  4.6 2.1 fusion.45
  6.7 2.0 collective-permute-start
  8.7 4.0 %reshape_reshape.3 = bf16[192,64,128]{2,1,0:T(8,128)(2,1)} reshape(bf16[192,2,4096]{2,1,0:T(2,128)(2,1)S(1)} %copy-done) | data formatting | bytes 6291456 | tf_op jit(solution)/shard_map/reshape;reshape | solution.py:45
  12.8 5.6 %copy.1789 = bf16[192,64,128]{2,0,1:T(8,128)(2,1)} copy(bf16[192,64,128]{2,1,0:T(8,128)(2,1)} %reshape_reshape.3) | data formatting | bytes 6291456 | tf_op jit(solution)/shard_map/reshape;reshape | solution.py:45
  18.4 13.8 %all-to-all-start = ((bf16[192,64,128]{2,0,1:T(8,128)(2,1)}), bf16[192,64,128]{2,0,1:T(8,128)(2,1)S(1)}, u32[]{:S(2)}, u32[]{:S(2)}) async-start(bf16[192,64,128]{2,0,1:T(8,128)(2,1)} %copy.1789), calls=%async_computation | async-start | bytes 6291456 | tf_op jit(solution)/shard_map/all_to_all | solution.py:49
  32.1 2.1 maximum_bitcast_fusion
  34.2 0.9 copy.1863
  35.6 2.0 fusion.43
  37.6 2.0 fusion.42
  67.6 2.0 fusion.41
  80.9 26.7 %all-to-all-done = bf16[192,64,128]{2,0,1:T(8,128)(2,1)S(1)} async-done(((bf16[192,64,128]{2,0,1:T(8,128)(2,1)}), bf16[192,64,128]{2,0,1:T(8,128)(2,1)S(1)}, u32[]{:S(2)}, u32[]{:S(2)}) %all-to-all-start) | async-done | bytes 3145760 | tf_op jit(solution)/shard_map/all_to_all | solution.py:49
  107.5 1.6 select_reduce_fusion.1
  110.5 5.3 %all-to-all-start.1 = ((f32[64,1,2]{2,1,0:T(1,128)}), f32[64,1,2]{2,1,0:T(1,128)S(1)}, u32[]{:S(2)}, u32[]{:S(2)}) async-start(f32[64,1,2]{2,1,0:T(1,128)} %broadcast_in_dim.31), calls=%async_computation.1 | async-start | bytes 65536 | tf_op jit(solution)/shard_map/all_to_all | solution.py:18
  116.4 9.7 %all-to-all-done.1 = f32[64,1,2]{2,1,0:T(1,128)S(1)} async-done(((f32[64,1,2]{2,1,0:T(1,128)}), f32[64,1,2]{2,1,0:T(1,128)S(1)}, u32[]{:S(2)}, u32[]{:S(2)}) %all-to-all-start.1) | async-done | bytes 544 | tf_op jit(solution)/shard_map/all_to_all | solution.py:18
  126.1 5.6 %all-to-all-start.2 = ((bf16[64,192,1,128]{3,1,2,0:T(8,128)(2,1)}), bf16[64,192,1,128]{3,1,2,0:T(8,128)(2,1)}, u32[]{:S(2)}, u32[]{:S(2)}) async-start(bf16[64,192,1,128]{3,1,2,0:T(8,128)(2,1)} %constant_dynamic-update-slice_fusion), calls=%async_computation.2 | async-start | bytes 6291456 | tf_op jit(solution)/shard_map/all_to_all | solution.py:51
  133.2 4.0 %collective-permute-start.1 = (f32[1,128,128]{1,2,0:T(8,128)S(1)}, f32[1,128,128]{1,2,0:T(8,128)S(1)}, u32[]{:S(2)}, u32[]{:S(2)}) collective-permute-start(f32[1,128,128]{1,2,0:T(8,128)S(1)} %bitcast.227), channel_id=1, source_target_pairs={{32,0},{33,1},{34,2},{35,3},{36,4},{37,5},{38,6},{39,7},{40,8},{41... | collective-permute-start | bytes 196616 | tf_op jit(solution)/shard_map/ppermute | solution.py:13
  137.2 4.5 %collective-permute-done.1 = f32[1,128,128]{1,2,0:T(8,128)S(1)} collective-permute-done((f32[1,128,128]{1,2,0:T(8,128)S(1)}, f32[1,128,128]{1,2,0:T(8,128)S(1)}, u32[]{:S(2)}, u32[]{:S(2)}) %collective-permute-start.1) | collective-permute-done | bytes 65568 | tf_op jit(solution)/shard_map/ppermute | solution.py:13
  141.8 11.7 %custom-call.10 = f32[1,128,128]{2,1,0:T(8,128)S(1)} custom-call(f32[1,128,128]{2,1,0:T(8,128)S(1)} %fusion.37), custom_call_target="Cholesky" | custom-call | tf_op jit(solution)/shard_map/vmap(jit(cholesky))/cholesky | solution.py:27
  154.9 9.8 %custom-call.11 = f32[1,1,128,128]{2,3,1,0:T(8,128)S(1)} custom-call(f32[1,1,128,128]{3,2,1,0:T(8,128)S(1)} %fusion.26), custom_call_target="InvertDiagBlocksLowerTriangular" | custom-call | tf_op jit(solution)/shard_map/vmap(jit(_cho_solve))/triangular_solve | solution.py:28
  164.7 39.2 %all-to-all-done.2 = bf16[64,192,1,128]{3,1,2,0:T(8,128)(2,1)} async-done(((bf16[64,192,1,128]{3,1,2,0:T(8,128)(2,1)}), bf16[64,192,1,128]{3,1,2,0:T(8,128)(2,1)}, u32[]{:S(2)}, u32[]{:S(2)}) %all-to-all-start.2) | async-done | bytes 3145760 | tf_op jit(solution)/shard_map/all_to_all | solution.py:51
  203.9 2.9 %fusion.21 = f32[128,128]{1,0:T(8,128)S(1)} fusion(bf16[192,64,128]{2,0,1:T(8,128)(2,1)S(1)} %all-to-all-done, bf16[64,192,1,128]{3,1,2,0:T(8,128)(2,1)} %all-to-all-done.2, pred[]{:T(512)S(6)} %and.11), kind=kOutput, calls=%fused_computation.12 | convolution fusion | flops 402685952 | bytes 6356993 | tf_op jit(solution)/shard_map/tgb,tgc->gbc/dot_general | solution.py:65
  207.9 11.7 %custom-call.12 = f32[1,128,128]{2,1,0:T(8,128)S(1)} custom-call(f32[1,128,128]{2,1,0:T(8,128)S(1)} %fusion.29), custom_call_target="Cholesky" | custom-call | tf_op jit(solution)/shard_map/vmap(jit(cholesky))/cholesky | solution.py:27
  220.9 9.8 %custom-call.13 = f32[1,1,128,128]{2,3,1,0:T(8,128)S(1)} custom-call(f32[1,1,128,128]{3,2,1,0:T(8,128)S(1)} %fusion.27), custom_call_target="InvertDiagBlocksLowerTriangular" | custom-call | tf_op jit(solution)/shard_map/vmap(jit(_cho_solve))/triangular_solve | solution.py:28
  (95 shorter events, 48.1 us)
Async XLA Ops:
  4.6 4.1 %copy-start = (bf16[192,2,4096]{2,1,0:T(2,128)(2,1)S(1)}, bf16[192,2,4096]{2,1,0:T(2,128)(2,1)}, u32[]{:S(2)}) copy-start(bf16[192,2,4096]{2,1,0:T(2,128)(2,1)} %param.5) | copy-start | bytes 9437188
  6.7 25.5 %collective-permute-start = (bf16[192,4096]{1,0:T(8,128)(2,1)}, bf16[192,4096]{1,0:T(8,128)(2,1)}, u32[]{:S(2)}, u32[]{:S(2)}) collective-permute-start(bf16[192,4096]{1,0:T(8,128)(2,1)} %get-tuple-element.139), channel_id=1, source_target_pairs={{64,0},{128,64},{192,128},{65,1},{129,65},{193,129},{66,2},{130,66... | collective-permute-start | bytes 4718600 | tf_op jit(solution)/shard_map/ppermute | solution.py:13
  18.4 89.2 %all-to-all-start = ((bf16[192,64,128]{2,0,1:T(8,128)(2,1)}), bf16[192,64,128]{2,0,1:T(8,128)(2,1)S(1)}, u32[]{:S(2)}, u32[]{:S(2)}) async-start(bf16[192,64,128]{2,0,1:T(8,128)(2,1)} %copy.1789), calls=%async_computation | async-start | bytes 6291456 | tf_op jit(solution)/shard_map/all_to_all | solution.py:49
  110.5 15.7 %all-to-all-start.1 = ((f32[64,1,2]{2,1,0:T(1,128)}), f32[64,1,2]{2,1,0:T(1,128)S(1)}, u32[]{:S(2)}, u32[]{:S(2)}) async-start(f32[64,1,2]{2,1,0:T(1,128)} %broadcast_in_dim.31), calls=%async_computation.1 | async-start | bytes 65536 | tf_op jit(solution)/shard_map/all_to_all | solution.py:18
  116.4 15.4 %copy-start.1 = (f32[2]{0:T(128)S(1)}, f32[2]{0:T(128)}, u32[]{:S(2)}) copy-start(f32[2]{0:T(128)} %param.6) | copy-start | bytes 28
  126.1 77.7 %all-to-all-start.2 = ((bf16[64,192,1,128]{3,1,2,0:T(8,128)(2,1)}), bf16[64,192,1,128]{3,1,2,0:T(8,128)(2,1)}, u32[]{:S(2)}, u32[]{:S(2)}) async-start(bf16[64,192,1,128]{3,1,2,0:T(8,128)(2,1)} %constant_dynamic-update-slice_fusion), calls=%async_computation.2 | async-start | bytes 6291456 | tf_op jit(solution)/shard_map/all_to_all | solution.py:51
  133.2 8.5 %collective-permute-start.1 = (f32[1,128,128]{1,2,0:T(8,128)S(1)}, f32[1,128,128]{1,2,0:T(8,128)S(1)}, u32[]{:S(2)}, u32[]{:S(2)}) collective-permute-start(f32[1,128,128]{1,2,0:T(8,128)S(1)} %bitcast.227), channel_id=1, source_target_pairs={{32,0},{33,1},{34,2},{35,3},{36,4},{37,5},{38,6},{39,7},{40,8},{41... | collective-permute-start | bytes 196616 | tf_op jit(solution)/shard_map/ppermute | solution.py:13
